TPU v7x, 32 devices: a whole 2x2x4 slice. The times are simulated.
32 devices in a mesh: inst: 4 (over x, core), dp: 4 (over z), tp: 2 (over y).
Axes of the slice: x: 2, y: 2, z: 4, core: 2. Of those that a mesh axis runs over, the one named last changes fastest.
Arguments:
- kernel_grads: bfloat16 [16, 2, 128, 4608], P(('inst', 'dp'), 'tp'), may hold values from -0.75 to 0.75
- kernel_master: float32 [2, 128, 4608], P('tp', 'dp'), may hold values from -6 to 6
- kernel_first: float32 [2, 128, 4608], P('tp', 'dp'), may hold values from -3 to 3
- kernel_second: float32 [2, 128, 4608], P('tp', 'dp'), may hold values from 0.05 to 4
- gain_grads: bfloat16 [32, 4, 4608], P(('inst', 'dp', 'tp')), may hold values from -0.29882812 to 0.29882812
- gain_master: float32 [4, 4608], replicated, may hold values from -6 to 6
- gain_first: float32 [4, 4608], replicated, may hold values from -3 to 3
- gain_second: float32 [4, 4608], replicated, may hold values from 0.05 to 4
Outputs:
- kernel_params: bfloat16 [2, 128, 4608], P('tp')
- kernel_master_new: float32 [2, 128, 4608], P('tp', 'dp')
- kernel_first_new: float32 [2, 128, 4608], P('tp', 'dp')
- kernel_second_new: float32 [2, 128, 4608], P('tp', 'dp')
- gain_params: bfloat16 [4, 4608], replicated
- gain_master_new: float32 [4, 4608], replicated
- gain_first_new: float32 [4, 4608], replicated
- gain_second_new: float32 [4, 4608], replicated
All inputs are finite; a program needn't handle non-finite values.
Results may differ from a plain program's by a relative error of at most 0.004.
Values may be sent and summed in bfloat16 or wider, within the bound.
A program may use at most 64 MiB of HBM per device.

v0:
```python
import jax
import jax.numpy as jnp
from jax import lax
from jax.sharding import PartitionSpec as P

beta_one = 0.9
beta_two = 0.95
learn_rate = 0.01
decay_rate = 0.1
epsilon = 1e-08
step_count = 100.0


def adam_update(gradient, master, first_moment, second_moment):
    first_next = beta_one * first_moment + (1.0 - beta_one) * gradient
    second_next = beta_two * second_moment + (1.0 - beta_two) * gradient * gradient
    first_hat = first_next / (1.0 - beta_one**step_count)
    second_hat = second_next / (1.0 - beta_two**step_count)
    master_next = master - learn_rate * (
        first_hat / (jnp.sqrt(second_hat) + epsilon) + decay_rate * master
    )
    return (master_next, first_next, second_next)


def local(
    kernel_grads,
    kernel_master,
    kernel_first,
    kernel_second,
    gain_grads,
    gain_master,
    gain_first,
    gain_second,
):
    local_grads = kernel_grads[0].astype(jnp.float32)
    gain_local = gain_grads[0].astype(jnp.float32)
    flat_grads = gain_local.reshape(-1)
    gain_whole = None
    partial_rows, gain_piece = (
        lax.psum_scatter(
            local_grads.astype(jnp.bfloat16), "dp", scatter_dimension=1, tiled=True
        ).astype(jnp.float32),
        lax.psum_scatter(
            flat_grads.astype(jnp.bfloat16), "dp", scatter_dimension=0, tiled=True
        ).astype(jnp.float32),
    )
    gradient, gain_piece = (
        lax.psum(partial_rows.astype(jnp.bfloat16), "inst").astype(jnp.float32),
        lax.psum(gain_piece.astype(jnp.bfloat16), "inst").astype(jnp.float32),
    )
    kernel_master_new, kernel_first_new, kernel_second_new = adam_update(
        gradient, kernel_master, kernel_first, kernel_second
    )
    kernel_params = lax.all_gather(kernel_master_new.astype(jnp.bfloat16), "dp", axis=1, tiled=True)
    gain_piece = lax.psum(gain_piece, "tp")
    gain_whole = lax.all_gather(gain_piece, "dp", axis=0, tiled=True).reshape(gain_master.shape)
    gain_master_new, gain_first_new, gain_second_new = adam_update(
        gain_whole, gain_master, gain_first, gain_second
    )
    gain_params = gain_master_new.astype(jnp.bfloat16)
    return (
        kernel_params,
        kernel_master_new,
        kernel_first_new,
        kernel_second_new,
        gain_params,
        gain_master_new,
        gain_first_new,
        gain_second_new,
    )


def solution(mesh):
    return jax.shard_map(
        local,
        mesh=mesh,
        in_specs=(
            P(("inst", "dp"), "tp", None, None),
            P("tp", "dp", None),
            P("tp", "dp", None),
            P("tp", "dp", None),
            P(("inst", "dp", "tp"), None, None),
            P(),
            P(),
            P(),
        ),
        out_specs=(
            P("tp", None, None),
            P("tp", "dp", None),
            P("tp", "dp", None),
            P("tp", "dp", None),
            P(),
            P(),
            P(),
            P(),
        ),
        check_vma=False,
    )
```

profile of v0, /device:TPU:0, one launch (start us, length us, event | category | flops | bytes accessed | tf_op | source)
XLA Modules:
  0.0 142.5 jit_solution(16182226304347898728)
XLA Ops:
  7.2 0.0 copy-start.1
  7.2 0.0 copy-start
  7.2 0.0 reduce-scatter.2.cloned.1.call-start
  7.2 0.7 reduce-scatter.2.cloned.1.call-update
  7.9 0.0 all-reduce.3.cloned.1.call-start
  8.0 34.4 %reduce-scatter.2.cloned.1.call-done = bf16[1,32,4608]{2,1,0:T(8,128)(2,1)} async-done(((bf16[1,128,4608]{2,1,0:T(8,128)(2,1)}), bf16[1,32,4608]{2,1,0:T(8,128)(2,1)}) %reduce-scatter.2.cloned.1.call-update) | async-done | bytes 294928 | tf_op jit(solution)/shard_map/reduce_scatter | solution.py:40
  42.4 0.0 all-reduce.3.cloned.1.call-update
  42.4 0.0 copy-start.5
  42.4 0.0 copy-start.6
  42.4 0.0 copy-start.2
  42.4 0.0 copy-start.3
  42.5 0.0 copy-start.4
  42.5 0.0 all-gather.3.cloned.1.call-start
  42.5 33.3 %all-reduce.3.cloned.1.call-done = bf16[1,32,4608]{2,1,0:T(8,128)(2,1)} async-done(((bf16[1,32,4608]{2,1,0:T(8,128)(2,1)}), bf16[1,32,4608]{2,1,0:T(8,128)(2,1)}) %all-reduce.3.cloned.1.call-update) | async-done | bytes 294928 | tf_op jit(solution)/shard_map/psum | solution.py:48
  75.8 0.0 copy-done.1
  75.8 0.0 copy-done
  75.8 2.7 %fusion.7 = (bf16[1,32,4608]{2,1,0:T(8,128)(2,1)}, f32[1,32,4608]{2,1,0:T(8,128)}, f32[1,32,4608]{2,1,0:T(8,128)}, f32[1,32,4608]{2,1,0:T(8,128)}) fusion(f32[1,32,4608]{2,1,0:T(8,128)S(1)} %copy-done, bf16[1,32,4608]{2,1,0:T(8,128)(2,1)} %all-reduce.3.cloned.1.call-done, f32[1,32,4608]{2,1,0:T(8,128)S(1)} %copy-done.1, f32[1,32,4608]{2,1,0:T(8,128)} %param.11), kind=kLoop, calls=%fused_computation.11 | loop fusion | flops 2506752 | bytes 4128768 | tf_op jit(solution)/shard_map/convert_element_type | solution.py:54
  78.5 0.0 all-gather.3.cloned.1.call-update
  78.6 0.0 copy-done.5
  78.6 0.0 copy-done.6
  78.6 0.6 dynamic-slice
  79.9 20.5 %all-reduce = bf16[18432]{0:T(1024)(128)(2,1)S(1)} all-reduce(bf16[18432]{0:T(1024)(128)(2,1)S(1)} %squeeze.7), channel_id=3, replica_groups=mesh['inst'=4,'dp'=4,'tp'=2] {'dp'}, use_global_device_ids=true, to_apply=%region_2.0.clone | all-reduce | flops 18432 | bytes 73728
  100.4 0.1 dynamic-slice.1
  100.5 10.9 %psum.22 = bf16[4608]{0:T(1024)(128)(2,1)S(1)} all-reduce(bf16[4608]{0:T(1024)(128)(2,1)S(1)} %dynamic-slice.1), channel_id=1, replica_groups=mesh['inst'=4,'dp'=4,'tp'=2] {'inst'}, use_global_device_ids=true, to_apply=%region_3.0 | all-reduce | flops 4608 | bytes 18432 | tf_op jit(solution)/shard_map/psum | solution.py:49
  111.4 8.2 %psum.23 = f32[4608]{0:T(1024)S(1)} all-reduce(bf16[4608]{0:T(1024)(128)(2,1)S(1)} %psum.22), channel_id=1, replica_groups=mesh['inst'=4,'dp'=4,'tp'=2] {'tp'}, use_global_device_ids=true, to_apply=%region_4.0 | all-reduce | flops 4608 | bytes 27648 | tf_op jit(solution)/shard_map/psum | solution.py:55
  119.6 13.2 %all-gather = f32[4,1,4608]{2,1,0:T(1,128)S(1)} all-gather(f32[1,1,4608]{2,1,0:T(1,128)S(1)} %reshape.22), channel_id=1, replica_groups=mesh['inst'=4,'dp'=4,'tp'=2] {'dp'}, dimensions={0}, use_global_device_ids=true | all-gather | bytes 92160 | tf_op jit(solution)/shard_map/all_gather | solution.py:56
  132.8 0.0 copy-done.2
  132.8 0.0 copy-done.3
  132.8 0.0 copy-done.4
  132.8 0.8 fusion.4
  133.6 0.0 all-gather.3.cloned.1.call-done
  133.6 2.4 %copy.23 = bf16[1,128,4608]{2,1,0:T(8,128)(2,1)} copy(bf16[1,128,4608]{2,1,0:T(8,128)(2,1)} %all-gather.3.cloned.1.call-done) | data formatting | bytes 2359296
  (2 shorter events, 0.0 us)
Async XLA Ops:
  7.2 68.6 %copy-start.1 = (f32[1,32,4608]{2,1,0:T(8,128)S(1)}, f32[1,32,4608]{2,1,0:T(8,128)}, u32[]{:S(2)}) copy-start(f32[1,32,4608]{2,1,0:T(8,128)} %param.10) | copy-start | bytes 1769476
  7.2 68.6 %copy-start = (f32[1,32,4608]{2,1,0:T(8,128)S(1)}, f32[1,32,4608]{2,1,0:T(8,128)}, u32[]{:S(2)}) copy-start(f32[1,32,4608]{2,1,0:T(8,128)} %param.9) | copy-start | bytes 1769476
  7.2 35.2 %reduce-scatter.2.cloned.1.call-start = ((), (), s32[]{:S(2)}) async-start(), calls=%async_computation.1 | async-start | bytes 1474560 | tf_op jit(solution)/shard_map/reduce_scatter | solution.py:40
  7.9 67.9 %all-reduce.3.cloned.1.call-start = ((), (), s32[]{:S(2)}) async-start(), calls=%async_computation.2 | async-start | bytes 589824 | tf_op jit(solution)/shard_map/psum | solution.py:48
  42.4 36.2 %copy-start.5 = (bf16[1,4,4608]{2,1,0:T(4,128)(2,1)S(1)}, bf16[1,4,4608]{2,1,0:T(4,128)(2,1)}, u32[]{:S(2)}) copy-start(bf16[1,4,4608]{2,1,0:T(4,128)(2,1)} %param.12) | copy-start | bytes 110596
  42.4 36.2 %copy-start.6 = (u32[32]{0:T(128)S(1)}, u32[32]{0:T(128)}, u32[]{:S(2)}) copy-start(u32[32]{0:T(128)} %constant.35) | copy-start | bytes 388
  42.4 90.3 %copy-start.2 = (f32[4,4608]{1,0:T(4,128)S(1)}, f32[4,4608]{1,0:T(4,128)}, u32[]{:S(2)}) copy-start(f32[4,4608]{1,0:T(4,128)} %param.13) | copy-start | bytes 221188
  42.4 90.3 %copy-start.3 = (f32[4,4608]{1,0:T(4,128)S(1)}, f32[4,4608]{1,0:T(4,128)}, u32[]{:S(2)}) copy-start(f32[4,4608]{1,0:T(4,128)} %param.14) | copy-start | bytes 221188
  42.5 90.3 %copy-start.4 = (f32[4,4608]{1,0:T(4,128)S(1)}, f32[4,4608]{1,0:T(4,128)}, u32[]{:S(2)}) copy-start(f32[4,4608]{1,0:T(4,128)} %param.15) | copy-start | bytes 221188
  42.5 91.1 %all-gather.3.cloned.1.call-start = ((), (), s32[]{:S(2)}) async-start(), calls=%async_computation.3 | async-start | bytes 1474560 | tf_op jit(solution)/shard_map/all_gather | solution.py:54
Sparse Core Ops, SparseCore 0:
  10.3 32.0 reduce-scatter.1
  44.7 31.0 all-reduce.2
  78.7 30.9 all-gather.2
where the time goes:
time: 143 us; the launch traced here: 142 us
  waiting for transfers between devices  68.4 us (48%)
  blocking collectives  52.8 us (37%)
  between operations  14.5 us (10%)
  other arithmetic  3.55 us (2%)
  local copies, waits for them, and re-layouts  3.1 us (2%)
    reduce_scatter x1, waiting for transfers between devices, local(): lax.psum_scatter(local_grads.astype(jnp.bfloat16), 'dp', scatter_dimensio...  34.4 us
    psum x1, waiting for transfers between devices, local(): lax.psum(partial_rows.astype(jnp.bfloat16), 'inst').astype(jnp.float32)  33.3 us
    unnamed x1, blocking collectives  20.5 us
    all_gather x1, blocking collectives, local(): lax.all_gather(gain_piece, 'dp', axis=0, tiled=True)  13.2 us
    psum x1, blocking collectives, local(): lax.psum(gain_piece.astype(jnp.bfloat16), 'inst').astype(jnp.float32)  10.9 us
    psum x1, blocking collectives, local(): gain_piece = lax.psum(gain_piece, 'tp')  8.21 us
    unnamed x18, local copies, waits for them, and re-layouts  3.08 us
  transfers between devices with their start and end apart: 3, of which 2 were waited for; matrix products, arithmetic and copies ran while one was open for 1% of the time, Pallas kernels for 0%

commit v1 on v0

--- a/solution.py
+++ b/solution.py
@@ -52,7 +52,7 @@
         gradient, kernel_master, kernel_first, kernel_second
     )
     kernel_params = lax.all_gather(kernel_master_new.astype(jnp.bfloat16), "dp", axis=1, tiled=True)
-    gain_piece = lax.psum(gain_piece, "tp")
+    gain_piece = jnp.sum(lax.all_gather(gain_piece, "tp"), axis=0)
     gain_whole = lax.all_gather(gain_piece, "dp", axis=0, tiled=True).reshape(gain_master.shape)
     gain_master_new, gain_first_new, gain_second_new = adam_update(
         gain_whole, gain_master, gain_first, gain_second

time: 143 us -> 119 us (0.83)
  waiting for transfers between devices: 68.4 us -> 51 us
  blocking collectives: 52.8 us -> 46.2 us
    psum x1, waiting for transfers between devices: 33.3 us -> 4.08 us  [local(): lax.psum(partial_rows.astype(jnp.bfloat16), 'inst').astype(jnp.float32)]
    all_gather x1, waiting for transfers between devices: 0.01 us -> 11.8 us  [local(): lax.all_gather(kernel_master_new.astype(jnp.bfloat16), 'dp', axis=1, tile...]
    psum x1 -> x0, blocking collectives: 8.21 us -> none  [local(): gain_piece = lax.psum(gain_piece, 'tp')]
    all_gather x0 -> x1, blocking collectives: none -> 4.43 us  [local(): gain_piece = jnp.sum(lax.all_gather(gain_piece, 'tp'), axis=0)]
    unnamed x1, blocking collectives: 20.5 us -> 17 us
  transfers between devices with their start and end apart: 3 -> 3, of which waited for: 2 -> 3; matrix products, arithmetic and copies ran while one was open for 1% -> 1% of each run, Pallas kernels for 0% -> 0%
where the time goes in v1:
time: 119 us
  waiting for transfers between devices  51 us (43%)
  blocking collectives  46.2 us (39%)
  between operations  14.5 us (12%)
  other arithmetic  3.62 us (3%)
  local copies, waits for them, and re-layouts  3.11 us (3%)
    reduce_scatter x1, waiting for transfers between devices, local(): lax.psum_scatter(local_grads.astype(jnp.bfloat16), 'dp', scatter_dimensio...  34.4 us
    unnamed x1, blocking collectives  17 us
    all_gather x1, blocking collectives, local(): lax.all_gather(gain_piece, 'dp', axis=0, tiled=True)  13.9 us
    all_gather x1, waiting for transfers between devices, local(): lax.all_gather(kernel_master_new.astype(jnp.bfloat16), 'dp', axis=1, tile...  11.8 us
    psum x1, blocking collectives, local(): lax.psum(gain_piece.astype(jnp.bfloat16), 'inst').astype(jnp.float32)  10.8 us
    all_gather x1, blocking collectives, local(): gain_piece = jnp.sum(lax.all_gather(gain_piece, 'tp'), axis=0)  4.43 us
    psum x1, waiting for transfers between devices, local(): lax.psum(partial_rows.astype(jnp.bfloat16), 'inst').astype(jnp.float32)  4.08 us
    unnamed x18, local copies, waits for them, and re-layouts  3.08 us
  transfers between devices with their start and end apart: 3, of which 3 were waited for; matrix products, arithmetic and copies ran while one was open for 1% of the time, Pallas kernels for 0%

profile of v1, /device:TPU:0, one launch (start us, length us, event | category | flops | bytes accessed | tf_op | source)
XLA Modules:
  0.0 118.5 jit_solution(13353519362853990028)
XLA Ops:
  7.2 0.0 copy-start.6
  7.2 0.0 copy-start.5
  7.2 0.0 copy-start.1
  7.2 0.0 copy-start
  7.2 0.0 reduce-scatter.2.cloned.1.call-start
  7.3 0.7 reduce-scatter.2.cloned.1.call-update
  7.9 0.0 all-reduce.3.cloned.1.call-start
  8.0 34.4 %reduce-scatter.2.cloned.1.call-done = bf16[1,32,4608]{2,1,0:T(8,128)(2,1)} async-done(((bf16[1,128,4608]{2,1,0:T(8,128)(2,1)}), bf16[1,32,4608]{2,1,0:T(8,128)(2,1)}) %reduce-scatter.2.cloned.1.call-update) | async-done | bytes 294928 | tf_op jit(solution)/shard_map/reduce_scatter | solution.py:40
  42.4 0.0 all-reduce.3.cloned.1.call-update
  42.4 0.0 all-gather.4.cloned.1.call-start
  42.5 0.0 copy-done.5
  42.5 0.0 copy-done.6
  42.5 0.6 dynamic-slice
  43.8 17.0 %all-reduce = bf16[18432]{0:T(1024)(128)(2,1)S(1)} all-reduce(bf16[18432]{0:T(1024)(128)(2,1)S(1)} %squeeze.7), channel_id=3, replica_groups=mesh['inst'=4,'dp'=4,'tp'=2] {'dp'}, use_global_device_ids=true, to_apply=%region_2.0.clone | all-reduce | flops 18432 | bytes 73728
  60.8 0.1 dynamic-slice.1
  60.9 10.8 %psum.15 = bf16[1,4608]{1,0:T(2,128)(2,1)S(1)} all-reduce(bf16[1,4608]{1,0:T(2,128)(2,1)S(1)} %all_gather.16), channel_id=1, replica_groups=mesh['inst'=4,'dp'=4,'tp'=2] {'inst'}, use_global_device_ids=true, to_apply=%region_3.0 | all-reduce | flops 4608 | bytes 18432 | tf_op jit(solution)/shard_map/psum | solution.py:49
  71.7 0.0 copy-start.2
  71.7 0.0 copy-start.3
  71.7 0.0 copy-start.4
  71.7 4.1 %all-reduce.3.cloned.1.call-done = bf16[1,32,4608]{2,1,0:T(8,128)(2,1)} async-done(((bf16[1,32,4608]{2,1,0:T(8,128)(2,1)}), bf16[1,32,4608]{2,1,0:T(8,128)(2,1)}) %all-reduce.3.cloned.1.call-update) | async-done | bytes 294928 | tf_op jit(solution)/shard_map/psum | solution.py:48
  75.8 0.0 copy-done.1
  75.8 0.0 copy-done
  75.8 2.7 %fusion.7 = (bf16[1,32,4608]{2,1,0:T(8,128)(2,1)}, f32[1,32,4608]{2,1,0:T(8,128)}, f32[1,32,4608]{2,1,0:T(8,128)}, f32[1,32,4608]{2,1,0:T(8,128)}) fusion(f32[1,32,4608]{2,1,0:T(8,128)S(1)} %copy-done, bf16[1,32,4608]{2,1,0:T(8,128)(2,1)} %all-reduce.3.cloned.1.call-done, f32[1,32,4608]{2,1,0:T(8,128)S(1)} %copy-done.1, f32[1,32,4608]{2,1,0:T(8,128)} %param.11), kind=kLoop, calls=%fused_computation.12 | loop fusion | flops 2506752 | bytes 4128768 | tf_op jit(solution)/shard_map/convert_element_type | solution.py:54
  78.6 0.0 all-gather.4.cloned.1.call-update
  78.6 4.4 %all-gather = f32[2,1,4608]{2,1,0:T(1,128)S(1)} all-gather(f32[1,1,4608]{2,1,0:T(1,128)S(1)} %bitcast_convert_fusion), channel_id=1, replica_groups=mesh['inst'=4,'dp'=4,'tp'=2] {'tp'}, dimensions={0}, use_global_device_ids=true | all-gather | bytes 55296 | tf_op jit(solution)/shard_map/all_gather | solution.py:55
  83.0 0.1 reduce_sum.9
  83.1 13.9 %all-gather.1 = f32[4,1,4608]{2,1,0:T(1,128)S(1)} all-gather(f32[1,1,4608]{2,1,0:T(1,128)S(1)} %reshape.24), channel_id=1, replica_groups=mesh['inst'=4,'dp'=4,'tp'=2] {'dp'}, dimensions={0}, use_global_device_ids=true | all-gather | bytes 92160 | tf_op jit(solution)/shard_map/all_gather | solution.py:56
  97.0 0.0 copy-done.2
  97.0 0.0 copy-done.3
  97.0 0.0 copy-done.4
  97.1 0.8 fusion.4
  97.9 11.8 %all-gather.4.cloned.1.call-done = bf16[1,128,4608]{2,1,0:T(8,128)(2,1)} async-done(((bf16[1,32,4608]{2,1,0:T(8,128)(2,1)}), bf16[1,128,4608]{2,1,0:T(8,128)(2,1)}) %all-gather.4.cloned.1.call-update) | async-done | bytes 1179664 | tf_op jit(solution)/shard_map/all_gather | solution.py:54
  109.6 2.4 %copy.23 = bf16[1,128,4608]{2,1,0:T(8,128)(2,1)} copy(bf16[1,128,4608]{2,1,0:T(8,128)(2,1)} %all-gather.4.cloned.1.call-done) | data formatting | bytes 2359296
  (4 shorter events, 0.1 us)
Async XLA Ops:
  7.2 35.4 %copy-start.6 = (u32[32]{0:T(128)S(1)}, u32[32]{0:T(128)}, u32[]{:S(2)}) copy-start(u32[32]{0:T(128)} %constant.37) | copy-start | bytes 388
  7.2 35.3 %copy-start.5 = (bf16[1,4,4608]{2,1,0:T(4,128)(2,1)S(1)}, bf16[1,4,4608]{2,1,0:T(4,128)(2,1)}, u32[]{:S(2)}) copy-start(bf16[1,4,4608]{2,1,0:T(4,128)(2,1)} %param.12) | copy-start | bytes 110596
  7.2 68.6 %copy-start.1 = (f32[1,32,4608]{2,1,0:T(8,128)S(1)}, f32[1,32,4608]{2,1,0:T(8,128)}, u32[]{:S(2)}) copy-start(f32[1,32,4608]{2,1,0:T(8,128)} %param.10) | copy-start | bytes 1769476
  7.2 68.6 %copy-start = (f32[1,32,4608]{2,1,0:T(8,128)S(1)}, f32[1,32,4608]{2,1,0:T(8,128)}, u32[]{:S(2)}) copy-start(f32[1,32,4608]{2,1,0:T(8,128)} %param.9) | copy-start | bytes 1769476
  7.2 35.2 %reduce-scatter.2.cloned.1.call-start = ((), (), s32[]{:S(2)}) async-start(), calls=%async_computation.1 | async-start | bytes 1474560 | tf_op jit(solution)/shard_map/reduce_scatter | solution.py:40
  7.9 67.9 %all-reduce.3.cloned.1.call-start = ((), (), s32[]{:S(2)}) async-start(), calls=%async_computation.2 | async-start | bytes 589824 | tf_op jit(solution)/shard_map/psum | solution.py:48
  42.4 67.2 %all-gather.4.cloned.1.call-start = ((), (), s32[]{:S(2)}) async-start(), calls=%async_computation.3 | async-start | bytes 1474560 | tf_op jit(solution)/shard_map/all_gather | solution.py:54
  71.7 25.3 %copy-start.2 = (f32[4,4608]{1,0:T(4,128)S(1)}, f32[4,4608]{1,0:T(4,128)}, u32[]{:S(2)}) copy-start(f32[4,4608]{1,0:T(4,128)} %param.13) | copy-start | bytes 221188
  71.7 25.3 %copy-start.3 = (f32[4,4608]{1,0:T(4,128)S(1)}, f32[4,4608]{1,0:T(4,128)}, u32[]{:S(2)}) copy-start(f32[4,4608]{1,0:T(4,128)} %param.14) | copy-start | bytes 221188
  71.7 25.3 %copy-start.4 = (f32[4,4608]{1,0:T(4,128)S(1)}, f32[4,4608]{1,0:T(4,128)}, u32[]{:S(2)}) copy-start(f32[4,4608]{1,0:T(4,128)} %param.15) | copy-start | bytes 221188
Sparse Core Ops, SparseCore 0:
  10.3 32.0 reduce-scatter.1
  44.7 31.0 all-reduce.2
  78.7 30.9 all-gather.3
